TPU v7x, 128 devices: a whole 4x4x4 slice. The times are simulated.
128 devices in a mesh: row: 16 (over y, x), col: 8 (over z, core).
Axes of the slice: x: 4, y: 4, z: 4, core: 2. Of those that a mesh axis runs over, the one named last changes fastest.
Arguments:
- a_window: float32 [16384, 8192], P('row', 'col'), may hold values from -6 to 6
- l_panel: float32 [16384, 1024], P('row'), may hold values from -0.1875 to 0.1875
- l_inverse: float32 [2, 512, 512], replicated, may hold values from -2 to 2, as said below
Outputs:
- reduced: float32 [16384, 8192], P('row', 'col')
Inputs may be any that keep to these rules, and one draw needn't show every extreme that they name: `l_inverse`: both blocks are lower triangular, with diagonal entries between 0.5 and 2.
All inputs are finite; a program needn't handle non-finite values.
Results may differ from a plain program's by a relative error of at most 0.000067.
Values sent between devices are 32-bit elements; how exact they have to be, the bound alone decides.
A program may use at most 128 MiB of HBM per device.

v0:
```python
import jax
import jax.numpy as jnp
from jax import lax
from jax.experimental import pallas as pl
from jax.experimental.pallas import tpu as pltpu
from jax.sharding import PartitionSpec as P

MESH = pl.DeviceIdType.MESH
F32 = jnp.float32
BF16 = jnp.bfloat16

W = 1024
HB = 512
RC = 8
KT = W // (4 * RC)
RP = 16
KP = W // (4 * RP)
RL = 32
KL = HB // (4 * RL)
ZR = 16
KZ = HB // ZR
KZL = HB // 2 // RL
SIG = 4
SZ = 3
S1 = 12
ZL0 = 32
ZG0 = 50
DEEP = 6


def split(v):
    hi = v.astype(BF16)
    return hi, (v - hi.astype(F32)).astype(BF16)


def nn(a, b):
    return jnp.dot(a, b, preferred_element_type=F32)


def nt(a, b):
    return lax.dot_general(a, b, (((1,), (1,)), ((), ())), preferred_element_type=F32)


def mul3(op, a, b):
    return op(a[0], b[0]) + (op(a[0], b[1]) + op(a[1], b[0]))


def wrap(v):
    return lax.rem(v + 4, 4)


class Tree:
    def __init__(self, t, x, y, root):
        rx, ry = lax.rem(root, 4), lax.div(root, 4)
        sgn = 1 if t % 2 == 0 else -1
        dx, dy = wrap((x - rx) * sgn), wrap((y - ry) * sgn)
        main, sec = (dx, dy) if t < 2 else (dy, dx)
        self.depth = jnp.where(main == 0, jnp.where(sec == 0, 0, sec + 2), main + sec)
        self.root = jnp.logical_and(main == 0, sec == 0)
        step = jnp.where(sec == 0, sgn, -sgn)
        self.has = (
            jnp.logical_or(
                jnp.logical_and(sec == 0, main < 3), jnp.logical_and(sec > 0, main == 1)
            ),
            jnp.logical_and(main >= 1, sec < 3),
        )
        if t < 2:
            self.to = (y * 4 + wrap(x + step), wrap(y + sgn) * 4 + x)
        else:
            self.to = (wrap(y + step) * 4 + x, y * 4 + wrap(x + sgn))


def kernel(
    a_hbm, l_hbm, inv_hbm, o_hbm,
    big, u, lr, inv, l10, gbuf, ph, plo, ah, al, lh, ll, ih, il, lth, ltl,
    load_sem, tree_recv, tree_send, l10_send,
    zr1, zr2, lr1, lr2, gr1, gr2, zsend, out_sem,
):
    row, col = lax.axis_index("row"), lax.axis_index("col")
    x, y = lax.rem(row, 4), lax.div(row, 4)
    z, core = lax.div(col, 2), lax.rem(col, 2)
    other = col + 1 - 2 * core
    top = row == 0

    def remote(src, dst, send, recv, to):
        return pltpu.make_async_remote_copy(
            src_ref=src, dst_ref=dst, send_sem=send, recv_sem=recv,
            device_id=to, device_id_type=MESH,
        )

    def rows_of(ref, at, n):
        return ref.at[pl.ds(pl.multiple_of(at, 8), n)]

    load_inv = pltpu.make_async_copy(inv_hbm, inv, load_sem.at[0])
    load_l = pltpu.make_async_copy(l_hbm, lr, load_sem.at[1])
    load_inv.start()
    load_l.start()

    barrier = pltpu.get_barrier_semaphore()
    peers = [
        (y * 4 + wrap(x + 1), col), (y * 4 + wrap(x - 1), col),
        (wrap(y + 1) * 4 + x, col), (wrap(y - 1) * 4 + x, col),
        (row, other),
        (row, 2 * wrap(z + 1) + core), (row, 2 * wrap(z - 1) + core),
        (row, 2 * wrap(z + jnp.where(core == 0, -1, 1)) + 1 - core),
    ]
    for peer in peers:
        pl.semaphore_signal(barrier, inc=1, device_id=peer, device_id_type=MESH)
    pl.semaphore_wait(barrier, len(peers))

    trees = [Tree(t, x, y, col) for t in range(4)]

    def split_inverse():
        load_inv.wait()
        for b in range(2):
            h, l = split(inv[b])
            ih[b] = h
            il[b] = l

    def split_coupling():
        h, l = split(l10[...])
        lth[...] = h
        ltl[...] = l

    def tree_step(t, k, at, buf, n, send):
        tree = trees[t]
        ref = rows_of(buf, at, n)

        @pl.when(jnp.logical_not(tree.root))
        def _():
            remote(ref, ref, send.at[t, 0], tree_recv.at[t, k], (row, col)).wait_recv()

        for s in range(2):
            @pl.when(tree.has[s])
            def _():
                remote(ref, ref, send.at[t, s], tree_recv.at[t, k], (tree.to[s], col)).start()

    def p_rows(at, n, eye):
        rows = pl.ds(pl.multiple_of(at, 8), n)
        l0, l1 = lr[rows, :HB], lr[rows, HB:]
        if eye:
            i = at + lax.broadcasted_iota(jnp.int32, (n, HB), 0)
            j = lax.broadcasted_iota(jnp.int32, (n, HB), 1)
            l0 = jnp.where(top, jnp.where(i == j, 1.0, 0.0), l0)
            l1 = jnp.where(top, jnp.where(i == j + HB, 1.0, 0.0), l1)
        p1 = split(mul3(nn, split(l1), (ih[1], il[1])))
        ph[rows, HB:] = p1[0]
        plo[rows, HB:] = p1[1]
        p0 = split(
            mul3(nn, split(l0 - mul3(nn, p1, (lth[...], ltl[...]))), (ih[0], il[0]))
        )
        ph[rows, :HB] = p0[0]
        plo[rows, :HB] = p0[1]

    def right_solve(r, put):
        x0 = mul3(nt, split(r[:, :HB]), (ih[0], il[0]))
        put(0, x0)
        mid = r[:, HB:] - mul3(nt, split(x0), (lth[...], ltl[...]))
        put(HB, mul3(nt, split(mid), (ih[1], il[1])))

    @pl.when(col == 0)
    def _():
        load_a = pltpu.make_async_copy(a_hbm, big.at[pl.ds(2 * W, W)], load_sem.at[2])
        load_a.start()
        load_c = pltpu.make_async_copy(
            l_hbm.at[pl.ds(HB, HB), pl.ds(0, HB)], l10, load_sem.at[3]
        )
        load_t = pltpu.make_async_copy(a_hbm, big.at[pl.ds(0, W)], load_sem.at[4])

        @pl.when(top)
        def _():
            load_c.start()
            load_t.start()
            load_c.wait()
            load_t.wait()

        load_a.wait()

        def send_a(k, _):
            for half, to in ((0, 2), (1, 7)):
                src = rows_of(big, 2 * W + half * HB + k * ZR, ZR)
                at = jnp.where(2 * to == 0, 0, 0) + 2 * W
                root = row == to
                dst = rows_of(big, jnp.where(root, W, at) + half * HB + k * ZR, ZR)
                remote(src, dst, zsend.at[0, half], zr1.at[k], (row, to)).start()

            @pl.when(row == 1)
            def _():
                for half, recv in ((0, zr2), (1, zr1)):
                    src = rows_of(big, 2 * W + half * HB + k * ZR, ZR)
                    dst = rows_of(big, W + half * HB + k * ZR, ZR)
                    remote(src, dst, zsend.at[0, 2 + half], recv.at[k], (row, 1)).start()
            return 0

        lax.fori_loop(0, KZ, send_a, 0)
        split_inverse()
        load_l.wait()

        def slot(s):
            for t in range(4):
                k = s - SIG * trees[t].depth

                @pl.when(jnp.logical_and(k >= 0, k < KL))
                def _():
                    tree_step(t, k, (k * 4 + t) * RL, l10, RL, l10_send)

                k2 = k - KL

                @pl.when(jnp.logical_and(k2 >= 0, k2 < KP))
                def _():
                    tree_step(t, k2 + KL, (k2 * 4 + t) * RP, big, RP, tree_send)

        first = KL + SIG * DEEP

        def comm_only(s, _):
            slot(s)
            return 0

        lax.fori_loop(0, first, comm_only, 0)

        def send_l(k, _):
            for half, to in ((0, 2), (1, 7)):
                ref = rows_of(l10, half * (HB // 2) + k * RL, RL)
                remote(ref, ref, zsend.at[1, half], lr1.at[k], (row, to)).start()
            for half, recv in ((0, lr2), (1, lr1)):
                ref = rows_of(l10, half * (HB // 2) + k * RL, RL)
                remote(ref, ref, zsend.at[1, 2 + half], recv.at[k], (row, 1)).start()
            return 0

        lax.fori_loop(0, KZL, send_l, 0)
        split_coupling()

        def with_p(i, _):
            slot(first + i)
            p_rows(i * 128, 128, True)
            return 0

        lax.fori_loop(0, 8, with_p, 0)
        lax.fori_loop(first + 8, KL + KP + SIG * DEEP, comm_only, 0)

        def split_a(i, _):
            rows = pl.ds(pl.multiple_of(i * 128, 128), 128)
            h, l = split(big[rows])
            ah[rows] = h
            al[rows] = l
            return 0

        lax.fori_loop(0, 8, split_a, 0)

        def block(g, _):
            half, q = lax.rem(g, 2), lax.div(g, 2)
            at = half * HB + q * 128
            rows = pl.ds(pl.multiple_of(at, 128), 128)
            p = (ph[rows], plo[rows])
            for n in range(2):
                cols = slice(n * HB, n * HB + HB)
                e = mul3(nn, p, (ah[:, cols], al[:, cols]))
                f = mul3(nt, p, (ah[cols], al[cols]))
                a = big[pl.ds(pl.multiple_of(2 * W + at, 128), 128), cols]
                u[rows, cols] = jnp.where(top, e, a - e)
                gbuf[rows, cols] = a - 0.5 * (e + f)

            def put_g(c0, v):
                gbuf[rows, c0:c0 + HB] = v

            right_solve(gbuf[rows], put_g)

            def put_o(c0, v):
                u[rows, c0:c0 + HB] = v

            right_solve(u[rows], put_o)

            def send_g(j, _):
                ref = rows_of(gbuf, at + j * ZR, ZR)
                k = q * (128 // ZR) + j

                @pl.when(half == 0)
                def _():
                    remote(ref, ref, zsend.at[2, 0], gr1.at[k], (row, 2)).start()
                    remote(ref, ref, zsend.at[2, 2], gr2.at[k], (row, 1)).start()

                @pl.when(half == 1)
                def _():
                    remote(ref, ref, zsend.at[2, 1], gr1.at[k], (row, 7)).start()
                    remote(ref, ref, zsend.at[2, 3], gr1.at[k], (row, 1)).start()
                return 0

            lax.fori_loop(0, 128 // ZR, send_g, 0)
            return 0

        lax.fori_loop(0, 8, block, 0)

        for t in range(4):
            for s in range(2):
                @pl.when(trees[t].has[s])
                def _():
                    ref = l10.at[pl.ds(0, KL * RL)]
                    remote(ref, ref, l10_send.at[t, s], lr1.at[0], (row, 1)).wait_send()
                    ref = big.at[pl.ds(0, KP * RP)]
                    remote(ref, ref, tree_send.at[t, s], lr1.at[0], (row, 1)).wait_send()
        for s in range(4):
            ref = big.at[pl.ds(0, HB)]
            if s < 2:
                remote(ref, ref, zsend.at[0, s], lr1.at[0], (row, 1)).wait_send()
            else:
                @pl.when(row == 1)
                def _():
                    remote(ref, ref, zsend.at[0, s], lr1.at[0], (row, 1)).wait_send()
            remote(ref, ref, zsend.at[2, s], lr1.at[0], (row, 1)).wait_send()
            ref = l10.at[pl.ds(0, HB // 2)]
            remote(ref, ref, zsend.at[1, s], lr1.at[0], (row, 1)).wait_send()

    @pl.when(col > 0)
    def _():
        load_u = pltpu.make_async_copy(a_hbm, u, load_sem.at[2])
        load_u.start()
        mine = row == col
        load_r = pltpu.make_async_copy(l_hbm, big.at[pl.ds(0, W)], load_sem.at[4])

        @pl.when(mine)
        def _():
            load_r.start()
            load_r.wait()

        start = jnp.where(col == 1, S1, 0)
        far = z > 0
        first_depth = jnp.where(far, jnp.where(core == 0, z, 4 - z), 1)
        second_depth = jnp.where(far, jnp.where(core == 0, 5 - z, z + 1), 1)
        on = jnp.where(core == 0, jnp.logical_and(far, z < 3), z > 1)
        nxt = jnp.where(core == 0, col + 2, col - 2)
        half = jnp.where(core == 0, 0, 1)

        def z_step(s, begin, count, ref_of, first, second, kind, only_root):
            k = s - begin - SZ * first_depth

            @pl.when(jnp.logical_and(k >= 0, k < count))
            def _():
                def go():
                    src = ref_of(col, half, k)
                    remote(src, src, zsend.at[kind, 0], first.at[k], (row, col)).wait_recv()

                    @pl.when(on)
                    def _():
                        remote(
                            src, ref_of(nxt, half, k), zsend.at[kind, 0], first.at[k], (row, nxt)
                        ).start()

                    @pl.when(jnp.logical_and(far, row == other) if only_root else far)
                    def _():
                        remote(
                            src, ref_of(other, half, k), zsend.at[kind, 1], second.at[k],
                            (row, other),
                        ).start()

                if only_root:
                    pl.when(jnp.logical_or(far, row == 1))(go)
                else:
                    go()

            k2 = s - begin - SZ * second_depth

            @pl.when(jnp.logical_and(k2 >= 0, k2 < count))
            def _():
                def go():
                    src = ref_of(col, 1 - half, k2)
                    remote(src, src, zsend.at[kind, 1], second.at[k2], (row, col)).wait_recv()

                if only_root:
                    pl.when(mine)(go)
                else:
                    go()

        def a_ref(c, h, k):
            base = jnp.where(row == c, W, 2 * W)
            return rows_of(big, base + h * HB + k * ZR, ZR)

        def l_ref(c, h, k):
            return rows_of(l10, h * (HB // 2) + k * RL, RL)

        def g_ref(c, h, k):
            return rows_of(gbuf, h * HB + k * ZR, ZR)

        def slot(s):
            z_step(s, 0, KZ, a_ref, zr1, zr2, 0, True)
            z_step(s, ZL0, KZL, l_ref, lr1, lr2, 1, False)
            z_step(s, ZG0, KZ, g_ref, gr1, gr2, 2, False)
            for t in range(4):
                k = s - start - SIG * trees[t].depth

                @pl.when(jnp.logical_and(k >= 0, k < 2 * KT))
                def _():
                    tree_step(t, k, (k * 4 + t) * RC, big, RC, tree_send)

        def comm_only(s, _):
            slot(s)
            return 0

        have_l = ZL0 + KZL + 4 * SZ
        lax.fori_loop(0, have_l, comm_only, 0)
        split_inverse()
        split_coupling()
        load_l.wait()

        def with_p(i, _):
            slot(have_l + i)
            p_rows(i * 128, 128, False)
            return 0

        lax.fori_loop(0, 8, with_p, 0)
        begin = 2 * KT + start
        lax.fori_loop(have_l + 8, begin, comm_only, 0)
        load_u.wait()

        def split_l(i, _):
            rows = pl.ds(pl.multiple_of(i * 128, 128), 128)
            h, l = split(big[rows])
            lh[rows] = h
            ll[rows] = l
            return 0

        lax.fori_loop(0, 8, split_l, 0)

        def with_update(v, _):
            slot(begin + v)
            b, w = lax.div(v, 8), lax.rem(v, 8)

            @pl.when(jnp.logical_and(w == 0, b < 4))
            def _():
                h, l = split(big[pl.ds(pl.multiple_of(W + b * 256, 256), 256)])
                ah[0:256] = h
                al[0:256] = l

            @pl.when(jnp.logical_and(w < 4, b < 4))
            def _():
                rows = pl.ds(pl.multiple_of(w * 256, 256), 256)
                cols = pl.ds(pl.multiple_of(b * 256, 256), 256)
                upd = mul3(nt, (ph[rows], plo[rows]), (ah[0:256], al[0:256]))
                u[rows, cols] = u[rows, cols] - jnp.where(top, 0.0, upd)

            @pl.when(jnp.logical_and(w >= 4, b > 0))
            def _():
                h = lax.rem(w, 2)
                c0 = lax.div(w - 4, 2) * HB
                at = h * HB + (b - 1) * 128
                rows = pl.ds(pl.multiple_of(at, 128), 128)
                cols = pl.ds(pl.multiple_of(c0, HB), HB)
                upd = mul3(nt, split(gbuf[rows]), (lh[cols], ll[cols]))
                u[rows, cols] = u[rows, cols] - jnp.where(top, 0.0, upd)
            return 0

        lax.fori_loop(0, 40, with_update, 0)

        for t in range(4):
            for s in range(2):
                @pl.when(trees[t].has[s])
                def _():
                    ref = big.at[pl.ds(0, 2 * KT * RC)]
                    remote(ref, ref, tree_send.at[t, s], lr1.at[0], (row, col)).wait_send()
        for kind in range(3):
            ref = l10.at[pl.ds(0, HB // 2)] if kind == 1 else big.at[pl.ds(0, HB)]

            @pl.when(on)
            def _():
                remote(ref, ref, zsend.at[kind, 0], lr1.at[0], (row, col)).wait_send()

            @pl.when(jnp.logical_and(far, row == other) if kind == 0 else far)
            def _():
                remote(ref, ref, zsend.at[kind, 1], lr1.at[0], (row, col)).wait_send()

    out = pltpu.make_async_copy(u, o_hbm, out_sem)
    out.start()
    out.wait()


def body(a_window, l_panel, l_inverse):
    vmem = pltpu.VMEM
    dma = pltpu.SemaphoreType.DMA
    return pl.pallas_call(
        kernel,
        out_shape=jax.ShapeDtypeStruct((W, W), F32),
        in_specs=[pl.BlockSpec(memory_space=pl.ANY)] * 3,
        out_specs=pl.BlockSpec(memory_space=pl.ANY),
        scratch_shapes=[
            vmem((3 * W, W), F32),
            vmem((W, W), F32),
            vmem((W, W), F32),
            vmem((2, HB, HB), F32),
            vmem((HB, HB), F32),
            vmem((W, W), F32),
            vmem((W, W), BF16), vmem((W, W), BF16),
            vmem((W, W), BF16), vmem((W, W), BF16),
            vmem((W, W), BF16), vmem((W, W), BF16),
            vmem((2, HB, HB), BF16), vmem((2, HB, HB), BF16),
            vmem((HB, HB), BF16), vmem((HB, HB), BF16),
            dma((5,)),
            dma((4, 2 * KT)),
            dma((4, 2)),
            dma((4, 2)),
            dma((KZ,)), dma((KZ,)),
            dma((KZL,)), dma((KZL,)),
            dma((KZ,)), dma((KZ,)),
            dma((3, 4)),
            dma,
        ],
        compiler_params=pltpu.CompilerParams(
            collective_id=0, has_side_effects=True, vmem_limit_bytes=64000000
        ),
        name="block_step",
    )(a_window, l_panel, l_inverse)


def solution(mesh):
    placed = (P("row", "col"), P("row", None), P())
    return jax.shard_map(
        body, mesh=mesh, in_specs=placed, out_specs=P("row", "col"), check_vma=False
    )
```

profile of v0, /device:TPU:1, one launch (start us, length us, event | category | flops | bytes accessed | tf_op | source)
XLA Modules:
  0.0 157.7 jit_solution(11454491583439421977)
XLA Ops:
  0.0 152.9 %block_step.1 = f32[1024,1024]{1,0:T(8,128)} custom-call(f32[1024,1024]{1,0:T(8,128)} %a_hbm.1, f32[1024,1024]{1,0:T(8,128)} %l_hbm.1, f32[2,512,512]{2,1,0:T(8,128)} %inv_hbm.1), custom_call_target="tpu_custom_call" | custom-call | tf_op jit(solution)/shard_map/block_step/pallas_call | solution.py:478
  152.9 4.8 %copy.5 = f32[1024,1024]{1,0:T(8,128)} copy(f32[1024,1024]{1,0:T(8,128)} %block_step.1) | data formatting | bytes 8388608
where the time goes:
time: 158 us
  Pallas kernels  153 us (97%)
  local copies, waits for them, and re-layouts  4.79 us (3%)
    pallas_call x1, Pallas kernels, body(): pl.pallas_call(kernel, out_shape=jax.ShapeDtypeStruct((W, W), F32), in_sp...  153 us
    unnamed x1, local copies, waits for them, and re-layouts  4.79 us

commit v1 on v0

--- a/solution.py
+++ b/solution.py
@@ -20,11 +20,12 @@
 ZR = 16
 KZ = HB // ZR
 KZL = HB // 2 // RL
-SIG = 4
-SZ = 3
-S1 = 12
-ZL0 = 32
-ZG0 = 50
+SIG = 6
+SP = 5
+SZ = 6
+SD = 2
+ZL0 = 36
+ZG0 = 56
 DEEP = 6
 
 
@@ -37,12 +38,8 @@
     return jnp.dot(a, b, preferred_element_type=F32)
 
 
-def nt(a, b):
-    return lax.dot_general(a, b, (((1,), (1,)), ((), ())), preferred_element_type=F32)
-
-
-def mul3(op, a, b):
-    return op(a[0], b[0]) + (op(a[0], b[1]) + op(a[1], b[0]))
+def mul3(a, b):
+    return nn(a[0], b[0]) + (nn(a[0], b[1]) + nn(a[1], b[0]))
 
 
 def wrap(v):
@@ -72,7 +69,7 @@
 
 def kernel(
     a_hbm, l_hbm, inv_hbm, o_hbm,
-    big, u, lr, inv, l10, gbuf, ph, plo, ah, al, lh, ll, ih, il, lth, ltl,
+    big, u, lr, inv, l10, gbuf, ph, plo, ah, al, lh, ll, ih, il, jh, jl, lth, ltl, mth, mtl,
     load_sem, tree_recv, tree_send, l10_send,
     zr1, zr2, lr1, lr2, gr1, gr2, zsend, out_sem,
 ):
@@ -143,20 +140,25 @@
             j = lax.broadcasted_iota(jnp.int32, (n, HB), 1)
             l0 = jnp.where(top, jnp.where(i == j, 1.0, 0.0), l0)
             l1 = jnp.where(top, jnp.where(i == j + HB, 1.0, 0.0), l1)
-        p1 = split(mul3(nn, split(l1), (ih[1], il[1])))
+        p1 = split(mul3(split(l1), (ih[1], il[1])))
         ph[rows, HB:] = p1[0]
         plo[rows, HB:] = p1[1]
         p0 = split(
-            mul3(nn, split(l0 - mul3(nn, p1, (lth[...], ltl[...]))), (ih[0], il[0]))
+            mul3(split(l0 - mul3(p1, (lth[...], ltl[...]))), (ih[0], il[0]))
         )
         ph[rows, :HB] = p0[0]
         plo[rows, :HB] = p0[1]
 
     def right_solve(r, put):
-        x0 = mul3(nt, split(r[:, :HB]), (ih[0], il[0]))
+        x0 = mul3(split(r[:, :HB]), (jh[0], jl[0]))
         put(0, x0)
-        mid = r[:, HB:] - mul3(nt, split(x0), (lth[...], ltl[...]))
-        put(HB, mul3(nt, split(mid), (ih[1], il[1])))
+        mid = r[:, HB:] - mul3(split(x0), (mth[...], mtl[...]))
+        put(HB, mul3(split(mid), (jh[1], jl[1])))
+
+    def out_copy(at, n, i):
+        return pltpu.make_async_copy(
+            u.at[pl.ds(at, n)], o_hbm.at[pl.ds(at, n)], out_sem.at[i]
+        )
 
     @pl.when(col == 0)
     def _():
@@ -174,15 +176,14 @@
             load_c.wait()
             load_t.wait()
 
-        load_a.wait()
-
         def send_a(k, _):
-            for half, to in ((0, 2), (1, 7)):
-                src = rows_of(big, 2 * W + half * HB + k * ZR, ZR)
-                at = jnp.where(2 * to == 0, 0, 0) + 2 * W
-                root = row == to
-                dst = rows_of(big, jnp.where(root, W, at) + half * HB + k * ZR, ZR)
-                remote(src, dst, zsend.at[0, half], zr1.at[k], (row, to)).start()
+            @pl.when(row >= 2)
+            def _():
+                for half, to in ((0, 2), (1, 7)):
+                    src = rows_of(big, 2 * W + half * HB + k * ZR, ZR)
+                    at = jnp.where(row == to, W, 2 * W)
+                    dst = rows_of(big, at + half * HB + k * ZR, ZR)
+                    remote(src, dst, zsend.at[0, half], zr1.at[k], (row, to)).start()
 
             @pl.when(row == 1)
             def _():
@@ -192,13 +193,10 @@
                     remote(src, dst, zsend.at[0, 2 + half], recv.at[k], (row, 1)).start()
             return 0
 
-        lax.fori_loop(0, KZ, send_a, 0)
-        split_inverse()
-        load_l.wait()
 
         def slot(s):
             for t in range(4):
-                k = s - SIG * trees[t].depth
+                k = s - SP * trees[t].depth
 
                 @pl.when(jnp.logical_and(k >= 0, k < KL))
                 def _():
@@ -210,13 +208,32 @@
                 def _():
                     tree_step(t, k2 + KL, (k2 * 4 + t) * RP, big, RP, tree_send)
 
-        first = KL + SIG * DEEP
+        first = KL + SP * DEEP
 
         def comm_only(s, _):
             slot(s)
             return 0
 
-        lax.fori_loop(0, first, comm_only, 0)
+        lax.fori_loop(0, 2, comm_only, 0)
+        load_a.wait()
+
+        def with_send(i, _):
+            slot(2 + i)
+
+            @pl.when(jnp.logical_and(row >= 1, row < 8))
+            def _():
+                lax.fori_loop(4 * i, 4 * i + 4, send_a, 0)
+            return 0
+
+        lax.fori_loop(0, KZ // 4, with_send, 0)
+        split_inverse()
+        lax.fori_loop(10, 12, comm_only, 0)
+        for b in range(2):
+            h, l = split(inv[b].T)
+            jh[b] = h
+            jl[b] = l
+        load_l.wait()
+        lax.fori_loop(12, first, comm_only, 0)
 
         def send_l(k, _):
             for half, to in ((0, 2), (1, 7)):
@@ -229,14 +246,78 @@
 
         lax.fori_loop(0, KZL, send_l, 0)
         split_coupling()
+        h, l = split(l10[...].T)
+        mth[...] = h
+        mtl[...] = l
 
         def with_p(i, _):
-            slot(first + i)
-            p_rows(i * 128, 128, True)
-            return 0
-
-        lax.fori_loop(0, 8, with_p, 0)
-        lax.fori_loop(first + 8, KL + KP + SIG * DEEP, comm_only, 0)
+            slot(first + 2 * i)
+            slot(first + 2 * i + 1)
+            p_rows(i * 256, 256, True)
+            return 0
+
+        lax.fori_loop(0, 4, with_p, 0)
+        lax.fori_loop(first + 8, KL + KP + SP * DEEP, comm_only, 0)
+
+        def split_t(i, _):
+            rows = pl.ds(pl.multiple_of(i * 128, 128), 128)
+            h, l = split(big[pl.ds(pl.multiple_of(i * 128, 128), 128)] + big[0:W, rows].T)
+            lh[rows] = h
+            ll[rows] = l
+            return 0
+
+        lax.fori_loop(0, 8, split_t, 0)
+
+        def place(g):
+            half, q = lax.rem(g, 2), lax.div(g, 2)
+            return half, q, half * HB + q * 128
+
+        def send_block(g):
+            half, q, at = place(g)
+
+            def send_g(j, _):
+                ref = rows_of(gbuf, at + j * ZR, ZR)
+                k = q * (128 // ZR) + j
+
+                @pl.when(half == 0)
+                def _():
+                    remote(ref, ref, zsend.at[2, 0], gr1.at[k], (row, 2)).start()
+                    remote(ref, ref, zsend.at[2, 2], gr2.at[k], (row, 1)).start()
+
+                @pl.when(half == 1)
+                def _():
+                    remote(ref, ref, zsend.at[2, 1], gr1.at[k], (row, 7)).start()
+                    remote(ref, ref, zsend.at[2, 3], gr1.at[k], (row, 1)).start()
+                return 0
+
+            lax.fori_loop(0, 128 // ZR, send_g, 0)
+
+        def g_block(g, _):
+            _, _, at = place(g)
+            rows = pl.ds(pl.multiple_of(at, 128), 128)
+            p = (ph[rows], plo[rows])
+
+            def part(n):
+                cols = slice(n * HB, n * HB + HB)
+                pt = mul3(p, (lh[:, cols], ll[:, cols]))
+                a = big[pl.ds(pl.multiple_of(2 * W + at, 128), 128), cols]
+                gbuf[rows, cols] = a - 0.5 * pt
+
+            part(0)
+
+            @pl.when(g > 0)
+            def _():
+                send_block(g - 1)
+
+            part(1)
+
+            def put_g(c0, v):
+                gbuf[rows, c0:c0 + HB] = v
+
+            right_solve(gbuf[rows], put_g)
+            return 0
+
+        lax.fori_loop(0, 8, g_block, 0)
 
         def split_a(i, _):
             rows = pl.ds(pl.multiple_of(i * 128, 128), 128)
@@ -246,49 +327,31 @@
             return 0
 
         lax.fori_loop(0, 8, split_a, 0)
-
-        def block(g, _):
-            half, q = lax.rem(g, 2), lax.div(g, 2)
-            at = half * HB + q * 128
-            rows = pl.ds(pl.multiple_of(at, 128), 128)
+        send_block(7)
+
+        def o_block(g, _):
+            rows = pl.ds(pl.multiple_of(g * 128, 128), 128)
             p = (ph[rows], plo[rows])
             for n in range(2):
                 cols = slice(n * HB, n * HB + HB)
-                e = mul3(nn, p, (ah[:, cols], al[:, cols]))
-                f = mul3(nt, p, (ah[cols], al[cols]))
-                a = big[pl.ds(pl.multiple_of(2 * W + at, 128), 128), cols]
+                e = mul3(p, (ah[:, cols], al[:, cols]))
+                a = big[pl.ds(pl.multiple_of(2 * W + g * 128, 128), 128), cols]
                 u[rows, cols] = jnp.where(top, e, a - e)
-                gbuf[rows, cols] = a - 0.5 * (e + f)
-
-            def put_g(c0, v):
-                gbuf[rows, c0:c0 + HB] = v
-
-            right_solve(gbuf[rows], put_g)
 
             def put_o(c0, v):
                 u[rows, c0:c0 + HB] = v
 
             right_solve(u[rows], put_o)
-
-            def send_g(j, _):
-                ref = rows_of(gbuf, at + j * ZR, ZR)
-                k = q * (128 // ZR) + j
-
-                @pl.when(half == 0)
-                def _():
-                    remote(ref, ref, zsend.at[2, 0], gr1.at[k], (row, 2)).start()
-                    remote(ref, ref, zsend.at[2, 2], gr2.at[k], (row, 1)).start()
-
-                @pl.when(half == 1)
-                def _():
-                    remote(ref, ref, zsend.at[2, 1], gr1.at[k], (row, 7)).start()
-                    remote(ref, ref, zsend.at[2, 3], gr1.at[k], (row, 1)).start()
-                return 0
-
-            lax.fori_loop(0, 128 // ZR, send_g, 0)
-            return 0
-
-        lax.fori_loop(0, 8, block, 0)
+            return 0
+
+        lax.fori_loop(0, 4, o_block, 0)
+        early = out_copy(0, HB, 0)
+        early.start()
+        lax.fori_loop(4, 8, o_block, 0)
+        late = out_copy(HB, HB, 1)
+        late.start()
+        early.wait()
+        late.wait()
 
         for t in range(4):
             for s in range(2):
@@ -300,12 +363,10 @@
                     remote(ref, ref, tree_send.at[t, s], lr1.at[0], (row, 1)).wait_send()
         for s in range(4):
             ref = big.at[pl.ds(0, HB)]
-            if s < 2:
+            @pl.when(jnp.logical_and(row >= 2, row < 8) if s < 2 else row == 1)
+            def _():
                 remote(ref, ref, zsend.at[0, s], lr1.at[0], (row, 1)).wait_send()
-            else:
-                @pl.when(row == 1)
-                def _():
-                    remote(ref, ref, zsend.at[0, s], lr1.at[0], (row, 1)).wait_send()
+
             remote(ref, ref, zsend.at[2, s], lr1.at[0], (row, 1)).wait_send()
             ref = l10.at[pl.ds(0, HB // 2)]
             remote(ref, ref, zsend.at[1, s], lr1.at[0], (row, 1)).wait_send()
@@ -322,16 +383,16 @@
             load_r.start()
             load_r.wait()
 
-        start = jnp.where(col == 1, S1, 0)
         far = z > 0
-        first_depth = jnp.where(far, jnp.where(core == 0, z, 4 - z), 1)
-        second_depth = jnp.where(far, jnp.where(core == 0, 5 - z, z + 1), 1)
+        zrow = jnp.logical_and(far, jnp.logical_and(row >= 2, row < 8))
+        first_slots = jnp.where(far, SZ * jnp.where(core == 0, z, 4 - z), SD)
+        second_slots = jnp.where(far, SZ * jnp.where(core == 0, 4 - z, z) + SD, SD)
         on = jnp.where(core == 0, jnp.logical_and(far, z < 3), z > 1)
         nxt = jnp.where(core == 0, col + 2, col - 2)
         half = jnp.where(core == 0, 0, 1)
 
         def z_step(s, begin, count, ref_of, first, second, kind, only_root):
-            k = s - begin - SZ * first_depth
+            k = s - begin - first_slots
 
             @pl.when(jnp.logical_and(k >= 0, k < count))
             def _():
@@ -353,11 +414,11 @@
                         ).start()
 
                 if only_root:
-                    pl.when(jnp.logical_or(far, row == 1))(go)
+                    pl.when(zrow)(go)
                 else:
                     go()
 
-            k2 = s - begin - SZ * second_depth
+            k2 = s - begin - second_slots
 
             @pl.when(jnp.logical_and(k2 >= 0, k2 < count))
             def _():
@@ -366,7 +427,7 @@
                     remote(src, src, zsend.at[kind, 1], second.at[k2], (row, col)).wait_recv()
 
                 if only_root:
-                    pl.when(mine)(go)
+                    pl.when(jnp.logical_and(zrow, mine))(go)
                 else:
                     go()
 
@@ -379,46 +440,63 @@
 
         def g_ref(c, h, k):
             return rows_of(gbuf, h * HB + k * ZR, ZR)
+
+        @pl.when(jnp.logical_and(mine, col == 1))
+        def _():
+            def arrive(k, _):
+                ref = rows_of(big, W + k * ZR, ZR)
+                remote(ref, ref, zsend.at[0, 0], zr1.at[k], (row, col)).wait_recv()
+                remote(ref, ref, zsend.at[0, 0], zr2.at[k], (row, col)).wait_recv()
+                return 0
+
+            lax.fori_loop(0, KZ, arrive, 0)
 
         def slot(s):
             z_step(s, 0, KZ, a_ref, zr1, zr2, 0, True)
             z_step(s, ZL0, KZL, l_ref, lr1, lr2, 1, False)
             z_step(s, ZG0, KZ, g_ref, gr1, gr2, 2, False)
             for t in range(4):
-                k = s - start - SIG * trees[t].depth
+                k = s - SIG * trees[t].depth
 
                 @pl.when(jnp.logical_and(k >= 0, k < 2 * KT))
                 def _():
-                    tree_step(t, k, (k * 4 + t) * RC, big, RC, tree_send)
+                    m, i = lax.div(k, KT), lax.rem(k, KT)
+                    at = m * W + (t // 2) * HB + i * 2 * RC + (t % 2) * RC
+                    tree_step(t, k, at, big, RC, tree_send)
 
         def comm_only(s, _):
             slot(s)
             return 0
 
-        have_l = ZL0 + KZL + 4 * SZ
-        lax.fori_loop(0, have_l, comm_only, 0)
+        have_l = ZL0 + KZL + 3 * SZ + SD
+        lax.fori_loop(0, 20, comm_only, 0)
         split_inverse()
+        lax.fori_loop(20, have_l, comm_only, 0)
         split_coupling()
         load_l.wait()
 
         def with_p(i, _):
-            slot(have_l + i)
-            p_rows(i * 128, 128, False)
-            return 0
-
-        lax.fori_loop(0, 8, with_p, 0)
-        begin = 2 * KT + start
-        lax.fori_loop(have_l + 8, begin, comm_only, 0)
+            slot(have_l + 2 * i)
+            slot(have_l + 2 * i + 1)
+            p_rows(i * 256, 256, False)
+            return 0
+
+        lax.fori_loop(0, 4, with_p, 0)
+        begin = KT + 8 + SIG * DEEP
+        assert begin == have_l + 12
         load_u.wait()
 
         def split_l(i, _):
-            rows = pl.ds(pl.multiple_of(i * 128, 128), 128)
-            h, l = split(big[rows])
-            lh[rows] = h
-            ll[rows] = l
-            return 0
-
-        lax.fori_loop(0, 8, split_l, 0)
+            slot(have_l + 8 + i)
+            for j in range(2):
+                at = i * 256 + j * 128
+                cols = pl.ds(pl.multiple_of(at, 128), 128)
+                h, l = split(big[pl.ds(pl.multiple_of(at, 128), 128)].T)
+                lh[:, cols] = h
+                ll[:, cols] = l
+            return 0
+
+        lax.fori_loop(0, 4, split_l, 0)
 
         def with_update(v, _):
             slot(begin + v)
@@ -426,29 +504,42 @@
 
             @pl.when(jnp.logical_and(w == 0, b < 4))
             def _():
-                h, l = split(big[pl.ds(pl.multiple_of(W + b * 256, 256), 256)])
-                ah[0:256] = h
-                al[0:256] = l
-
-            @pl.when(jnp.logical_and(w < 4, b < 4))
-            def _():
-                rows = pl.ds(pl.multiple_of(w * 256, 256), 256)
-                cols = pl.ds(pl.multiple_of(b * 256, 256), 256)
-                upd = mul3(nt, (ph[rows], plo[rows]), (ah[0:256], al[0:256]))
-                u[rows, cols] = u[rows, cols] - jnp.where(top, 0.0, upd)
-
-            @pl.when(jnp.logical_and(w >= 4, b > 0))
-            def _():
-                h = lax.rem(w, 2)
-                c0 = lax.div(w - 4, 2) * HB
-                at = h * HB + (b - 1) * 128
+                for j in range(2):
+                    at = W + j * HB + b * 128
+                    h, l = split(big[pl.ds(pl.multiple_of(at, 128), 128)].T)
+                    ah[:, j * 128:j * 128 + 128] = h
+                    al[:, j * 128:j * 128 + 128] = l
+
+            @pl.when(jnp.logical_and(jnp.logical_or(w == 1, w == 3), b < 4))
+            def _():
+                rows = pl.ds(pl.multiple_of(lax.div(w, 2) * HB, HB), HB)
+                upd = mul3((ph[rows], plo[rows]), (ah[:, 0:256], al[:, 0:256]))
+                for j in range(2):
+                    cols = pl.ds(pl.multiple_of(j * HB + b * 128, 128), 128)
+                    part = jnp.where(top, 0.0, upd[:, j * 128:j * 128 + 128])
+                    u[rows, cols] = u[rows, cols] - part
+
+            @pl.when(jnp.logical_and(jnp.logical_or(w == 5, w == 7), b > 0))
+            def _():
+                at = lax.div(w - 5, 2) * HB + (b - 1) * 128
                 rows = pl.ds(pl.multiple_of(at, 128), 128)
-                cols = pl.ds(pl.multiple_of(c0, HB), HB)
-                upd = mul3(nt, split(gbuf[rows]), (lh[cols], ll[cols]))
-                u[rows, cols] = u[rows, cols] - jnp.where(top, 0.0, upd)
-            return 0
-
-        lax.fori_loop(0, 40, with_update, 0)
+                g = split(gbuf[rows])
+                for j in range(2):
+                    cols = slice(j * HB, j * HB + HB)
+                    upd = mul3(g, (lh[:, cols], ll[:, cols]))
+                    u[rows, cols] = u[rows, cols] - jnp.where(top, 0.0, upd)
+            return 0
+
+        lax.fori_loop(0, 32, with_update, 0)
+        early = [out_copy(h * HB, 384, h) for h in range(2)]
+        for c in early:
+            c.start()
+        lax.fori_loop(32, 40, with_update, 0)
+        late = [out_copy(h * HB + 384, 128, 2 + h) for h in range(2)]
+        for c in late:
+            c.start()
+        for c in early + late:
+            c.wait()
 
         for t in range(4):
             for s in range(2):
@@ -459,17 +550,13 @@
         for kind in range(3):
             ref = l10.at[pl.ds(0, HB // 2)] if kind == 1 else big.at[pl.ds(0, HB)]
 
-            @pl.when(on)
+            @pl.when(jnp.logical_and(zrow, on) if kind == 0 else on)
             def _():
                 remote(ref, ref, zsend.at[kind, 0], lr1.at[0], (row, col)).wait_send()
 
-            @pl.when(jnp.logical_and(far, row == other) if kind == 0 else far)
+            @pl.when(jnp.logical_and(zrow, row == other) if kind == 0 else far)
             def _():
                 remote(ref, ref, zsend.at[kind, 1], lr1.at[0], (row, col)).wait_send()
-
-    out = pltpu.make_async_copy(u, o_hbm, out_sem)
-    out.start()
-    out.wait()
 
 
 def body(a_window, l_panel, l_inverse):
@@ -491,6 +578,8 @@
             vmem((W, W), BF16), vmem((W, W), BF16),
             vmem((W, W), BF16), vmem((W, W), BF16),
             vmem((2, HB, HB), BF16), vmem((2, HB, HB), BF16),
+            vmem((2, HB, HB), BF16), vmem((2, HB, HB), BF16),
+            vmem((HB, HB), BF16), vmem((HB, HB), BF16),
             vmem((HB, HB), BF16), vmem((HB, HB), BF16),
             dma((5,)),
             dma((4, 2 * KT)),
@@ -500,7 +589,7 @@
             dma((KZL,)), dma((KZL,)),
             dma((KZ,)), dma((KZ,)),
             dma((3, 4)),
-            dma,
+            dma((4,)),
         ],
         compiler_params=pltpu.CompilerParams(
             collective_id=0, has_side_effects=True, vmem_limit_bytes=64000000

time: 158 us -> 115 us (0.73)
  Pallas kernels: 153 us -> 110 us
    pallas_call x1, Pallas kernels: 153 us -> 110 us  [body(): pl.pallas_call(kernel, out_shape=jax.ShapeDtypeStruct((W, W), F32), in_sp...]
where the time goes in v1:
time: 115 us
  Pallas kernels  110 us (96%)
  local copies, waits for them, and re-layouts  4.79 us (4%)
    pallas_call x1, Pallas kernels, body(): pl.pallas_call(kernel, out_shape=jax.ShapeDtypeStruct((W, W), F32), in_sp...  110 us
    unnamed x1, local copies, waits for them, and re-layouts  4.79 us

profile of v1, /device:TPU:1, one launch (start us, length us, event | category | flops | bytes accessed | tf_op | source)
XLA Modules:
  0.0 114.6 jit_solution(2498534505472838224)
XLA Ops:
  0.0 109.8 %block_step.1 = f32[1024,1024]{1,0:T(8,128)} custom-call(f32[1024,1024]{1,0:T(8,128)} %a_hbm.1, f32[1024,1024]{1,0:T(8,128)} %l_hbm.1, f32[2,512,512]{2,1,0:T(8,128)} %inv_hbm.1), custom_call_target="tpu_custom_call" | custom-call | tf_op jit(solution)/shard_map/block_step/pallas_call | solution.py:565
  109.8 4.8 %copy.5 = f32[1024,1024]{1,0:T(8,128)} copy(f32[1024,1024]{1,0:T(8,128)} %block_step.1) | data formatting | bytes 8388608

commit v2 on v1

--- a/solution.py
+++ b/solution.py
@@ -13,20 +13,22 @@
 HB = 512
 RC = 8
 KT = W // (4 * RC)
-RP = 16
+RP = 8
 KP = W // (4 * RP)
-RL = 32
+RL = 16
 KL = HB // (4 * RL)
 ZR = 16
 KZ = HB // ZR
-KZL = HB // 2 // RL
+RZ = 32
+KZL = HB // 2 // RZ
 SIG = 6
-SP = 5
+SP = 9
 SZ = 6
 SD = 2
 ZL0 = 36
-ZG0 = 56
+ZG0 = 62
 DEEP = 6
+HOLD = 56
 
 
 def split(v):
@@ -68,10 +70,10 @@
 
 
 def kernel(
-    a_hbm, l_hbm, inv_hbm, o_hbm,
-    big, u, lr, inv, l10, gbuf, ph, plo, ah, al, lh, ll, ih, il, jh, jl, lth, ltl, mth, mtl,
+    a_hbm, l_hbm, inv, u,
+    big, lr, l10, gbuf, ph, plo, ah, al, lh, ll, ih, il, jh, jl, lth, ltl, mth, mtl,
     load_sem, tree_recv, tree_send, l10_send,
-    zr1, zr2, lr1, lr2, gr1, gr2, zsend, out_sem,
+    zr1, zr2, lr1, lr2, gr1, gr2, zsend,
 ):
     row, col = lax.axis_index("row"), lax.axis_index("col")
     x, y = lax.rem(row, 4), lax.div(row, 4)
@@ -88,9 +90,34 @@
     def rows_of(ref, at, n):
         return ref.at[pl.ds(pl.multiple_of(at, 8), n)]
 
-    load_inv = pltpu.make_async_copy(inv_hbm, inv, load_sem.at[0])
     load_l = pltpu.make_async_copy(l_hbm, lr, load_sem.at[1])
-    load_inv.start()
+    load_a = pltpu.make_async_copy(a_hbm, big.at[pl.ds(2 * W, W)], load_sem.at[2])
+    load_u = pltpu.make_async_copy(a_hbm, u, load_sem.at[2])
+    load_c = pltpu.make_async_copy(
+        l_hbm.at[pl.ds(HB, HB), pl.ds(0, HB)], l10, load_sem.at[3]
+    )
+    load_t = pltpu.make_async_copy(a_hbm, big.at[pl.ds(0, W)], load_sem.at[4])
+    load_r = pltpu.make_async_copy(l_hbm, big.at[pl.ds(0, W)], load_sem.at[4])
+    panel = col == 0
+    mine = row == col
+
+    @pl.when(jnp.logical_and(mine, panel))
+    def _():
+        load_c.start()
+        load_t.start()
+
+    @pl.when(jnp.logical_and(mine, jnp.logical_not(panel)))
+    def _():
+        load_r.start()
+
+    @pl.when(panel)
+    def _():
+        load_a.start()
+
+    @pl.when(jnp.logical_not(panel))
+    def _():
+        load_u.start()
+
     load_l.start()
 
     barrier = pltpu.get_barrier_semaphore()
@@ -108,7 +135,6 @@
     trees = [Tree(t, x, y, col) for t in range(4)]
 
     def split_inverse():
-        load_inv.wait()
         for b in range(2):
             h, l = split(inv[b])
             ih[b] = h
@@ -155,24 +181,10 @@
         mid = r[:, HB:] - mul3(split(x0), (mth[...], mtl[...]))
         put(HB, mul3(split(mid), (jh[1], jl[1])))
 
-    def out_copy(at, n, i):
-        return pltpu.make_async_copy(
-            u.at[pl.ds(at, n)], o_hbm.at[pl.ds(at, n)], out_sem.at[i]
-        )
-
     @pl.when(col == 0)
     def _():
-        load_a = pltpu.make_async_copy(a_hbm, big.at[pl.ds(2 * W, W)], load_sem.at[2])
-        load_a.start()
-        load_c = pltpu.make_async_copy(
-            l_hbm.at[pl.ds(HB, HB), pl.ds(0, HB)], l10, load_sem.at[3]
-        )
-        load_t = pltpu.make_async_copy(a_hbm, big.at[pl.ds(0, W)], load_sem.at[4])
-
         @pl.when(top)
         def _():
-            load_c.start()
-            load_t.start()
             load_c.wait()
             load_t.wait()
 
@@ -214,33 +226,39 @@
             slot(s)
             return 0
 
-        lax.fori_loop(0, 2, comm_only, 0)
+        lax.fori_loop(0, 4, comm_only, 0)
         load_a.wait()
 
         def with_send(i, _):
-            slot(2 + i)
-
-            @pl.when(jnp.logical_and(row >= 1, row < 8))
-            def _():
-                lax.fori_loop(4 * i, 4 * i + 4, send_a, 0)
-            return 0
-
-        lax.fori_loop(0, KZ // 4, with_send, 0)
+            slot(4 + i)
+
+            @pl.when(jnp.logical_and(row >= 2, row < 8))
+            def _():
+                lax.fori_loop(2 * i, 2 * i + 2, send_a, 0)
+            return 0
+
+        lax.fori_loop(0, KZ // 2, with_send, 0)
         split_inverse()
-        lax.fori_loop(10, 12, comm_only, 0)
+        lax.fori_loop(20, 24, comm_only, 0)
         for b in range(2):
             h, l = split(inv[b].T)
             jh[b] = h
             jl[b] = l
         load_l.wait()
-        lax.fori_loop(12, first, comm_only, 0)
+        lax.fori_loop(24, HOLD, comm_only, 0)
+
+        @pl.when(row == 1)
+        def _():
+            lax.fori_loop(0, KZ, send_a, 0)
+
+        lax.fori_loop(HOLD, first, comm_only, 0)
 
         def send_l(k, _):
             for half, to in ((0, 2), (1, 7)):
-                ref = rows_of(l10, half * (HB // 2) + k * RL, RL)
+                ref = rows_of(l10, half * (HB // 2) + k * RZ, RZ)
                 remote(ref, ref, zsend.at[1, half], lr1.at[k], (row, to)).start()
             for half, recv in ((0, lr2), (1, lr1)):
-                ref = rows_of(l10, half * (HB // 2) + k * RL, RL)
+                ref = rows_of(l10, half * (HB // 2) + k * RZ, RZ)
                 remote(ref, ref, zsend.at[1, 2 + half], recv.at[k], (row, 1)).start()
             return 0
 
@@ -251,13 +269,13 @@
         mtl[...] = l
 
         def with_p(i, _):
-            slot(first + 2 * i)
-            slot(first + 2 * i + 1)
-            p_rows(i * 256, 256, True)
-            return 0
-
-        lax.fori_loop(0, 4, with_p, 0)
-        lax.fori_loop(first + 8, KL + KP + SP * DEEP, comm_only, 0)
+            for j in range(4):
+                slot(first + 4 * i + j)
+            p_rows(i * 128, 128, True)
+            return 0
+
+        lax.fori_loop(0, 8, with_p, 0)
+        lax.fori_loop(first + 32, KL + KP + SP * DEEP, comm_only, 0)
 
         def split_t(i, _):
             rows = pl.ds(pl.multiple_of(i * 128, 128), 128)
@@ -345,14 +363,7 @@
             return 0
 
         lax.fori_loop(0, 4, o_block, 0)
-        early = out_copy(0, HB, 0)
-        early.start()
         lax.fori_loop(4, 8, o_block, 0)
-        late = out_copy(HB, HB, 1)
-        late.start()
-        early.wait()
-        late.wait()
-
         for t in range(4):
             for s in range(2):
                 @pl.when(trees[t].has[s])
@@ -371,16 +382,18 @@
             ref = l10.at[pl.ds(0, HB // 2)]
             remote(ref, ref, zsend.at[1, s], lr1.at[0], (row, 1)).wait_send()
 
-    @pl.when(col > 0)
-    def _():
-        load_u = pltpu.make_async_copy(a_hbm, u, load_sem.at[2])
-        load_u.start()
-        mine = row == col
-        load_r = pltpu.make_async_copy(l_hbm, big.at[pl.ds(0, W)], load_sem.at[4])
+    def trailing(one):
+        rc, sig = (16, 5) if one else (RC, SIG)
+        kt = W // (4 * rc)
+        zl0, zg0 = (4, 30) if one else (ZL0, ZG0)
+        have_l = zl0 + KZL + (SD if one else 3 * SZ + SD)
+        begin = kt + kt // 4 + sig * DEEP
+        lag = 0 if one else 1
+        per = kt // 4
+        a_at, g_at = ((0, 1), (2, 3)) if one else ((1, 3), (5, 7))
 
         @pl.when(mine)
         def _():
-            load_r.start()
             load_r.wait()
 
         far = z > 0
@@ -436,42 +449,44 @@
             return rows_of(big, base + h * HB + k * ZR, ZR)
 
         def l_ref(c, h, k):
-            return rows_of(l10, h * (HB // 2) + k * RL, RL)
+            return rows_of(l10, h * (HB // 2) + k * RZ, RZ)
 
         def g_ref(c, h, k):
             return rows_of(gbuf, h * HB + k * ZR, ZR)
 
-        @pl.when(jnp.logical_and(mine, col == 1))
-        def _():
-            def arrive(k, _):
-                ref = rows_of(big, W + k * ZR, ZR)
-                remote(ref, ref, zsend.at[0, 0], zr1.at[k], (row, col)).wait_recv()
-                remote(ref, ref, zsend.at[0, 0], zr2.at[k], (row, col)).wait_recv()
-                return 0
-
-            lax.fori_loop(0, KZ, arrive, 0)
+        if one:
+            @pl.when(mine)
+            def _():
+                def arrive(k, _):
+                    ref = rows_of(big, W + k * ZR, ZR)
+                    remote(ref, ref, zsend.at[0, 0], zr1.at[k], (row, col)).wait_recv()
+                    remote(ref, ref, zsend.at[0, 0], zr2.at[k], (row, col)).wait_recv()
+                    return 0
+
+                lax.fori_loop(0, KZ, arrive, 0)
 
         def slot(s):
-            z_step(s, 0, KZ, a_ref, zr1, zr2, 0, True)
-            z_step(s, ZL0, KZL, l_ref, lr1, lr2, 1, False)
-            z_step(s, ZG0, KZ, g_ref, gr1, gr2, 2, False)
+            if not one:
+                z_step(s, 0, KZ, a_ref, zr1, zr2, 0, True)
+            z_step(s, zl0, KZL, l_ref, lr1, lr2, 1, False)
+            z_step(s, zg0, KZ, g_ref, gr1, gr2, 2, False)
             for t in range(4):
-                k = s - SIG * trees[t].depth
-
-                @pl.when(jnp.logical_and(k >= 0, k < 2 * KT))
+                k = s - sig * trees[t].depth
+
+                @pl.when(jnp.logical_and(k >= 0, k < 2 * kt))
                 def _():
-                    m, i = lax.div(k, KT), lax.rem(k, KT)
-                    at = m * W + (t // 2) * HB + i * 2 * RC + (t % 2) * RC
-                    tree_step(t, k, at, big, RC, tree_send)
+                    m, i = lax.div(k, kt), lax.rem(k, kt)
+                    at = m * W + (t // 2) * HB + i * 2 * rc + (t % 2) * rc
+                    tree_step(t, k, at, big, rc, tree_send)
 
         def comm_only(s, _):
             slot(s)
             return 0
 
-        have_l = ZL0 + KZL + 3 * SZ + SD
-        lax.fori_loop(0, 20, comm_only, 0)
+        early = min(20, have_l)
+        lax.fori_loop(0, early, comm_only, 0)
         split_inverse()
-        lax.fori_loop(20, have_l, comm_only, 0)
+        lax.fori_loop(early, have_l, comm_only, 0)
         split_coupling()
         load_l.wait()
 
@@ -482,12 +497,12 @@
             return 0
 
         lax.fori_loop(0, 4, with_p, 0)
-        begin = KT + 8 + SIG * DEEP
-        assert begin == have_l + 12
+        assert have_l + 12 <= begin
+        lax.fori_loop(have_l + 8, begin - 4, comm_only, 0)
         load_u.wait()
 
         def split_l(i, _):
-            slot(have_l + 8 + i)
+            slot(begin - 4 + i)
             for j in range(2):
                 at = i * 256 + j * 128
                 cols = pl.ds(pl.multiple_of(at, 128), 128)
@@ -500,7 +515,7 @@
 
         def with_update(v, _):
             slot(begin + v)
-            b, w = lax.div(v, 8), lax.rem(v, 8)
+            b, w = lax.div(v, per), lax.rem(v, per)
 
             @pl.when(jnp.logical_and(w == 0, b < 4))
             def _():
@@ -510,18 +525,20 @@
                     ah[:, j * 128:j * 128 + 128] = h
                     al[:, j * 128:j * 128 + 128] = l
 
-            @pl.when(jnp.logical_and(jnp.logical_or(w == 1, w == 3), b < 4))
-            def _():
-                rows = pl.ds(pl.multiple_of(lax.div(w, 2) * HB, HB), HB)
+            @pl.when(jnp.logical_and(jnp.logical_or(w == a_at[0], w == a_at[1]), b < 4))
+            def _():
+                rows = pl.ds(pl.multiple_of(jnp.where(w == a_at[1], HB, 0), HB), HB)
                 upd = mul3((ph[rows], plo[rows]), (ah[:, 0:256], al[:, 0:256]))
                 for j in range(2):
                     cols = pl.ds(pl.multiple_of(j * HB + b * 128, 128), 128)
                     part = jnp.where(top, 0.0, upd[:, j * 128:j * 128 + 128])
                     u[rows, cols] = u[rows, cols] - part
 
-            @pl.when(jnp.logical_and(jnp.logical_or(w == 5, w == 7), b > 0))
-            def _():
-                at = lax.div(w - 5, 2) * HB + (b - 1) * 128
+            gb = b - lag
+
+            @pl.when(jnp.logical_and(jnp.logical_or(w == g_at[0], w == g_at[1]), gb >= 0))
+            def _():
+                at = jnp.where(w == g_at[1], HB, 0) + gb * 128
                 rows = pl.ds(pl.multiple_of(at, 128), 128)
                 g = split(gbuf[rows])
                 for j in range(2):
@@ -530,22 +547,12 @@
                     u[rows, cols] = u[rows, cols] - jnp.where(top, 0.0, upd)
             return 0
 
-        lax.fori_loop(0, 32, with_update, 0)
-        early = [out_copy(h * HB, 384, h) for h in range(2)]
-        for c in early:
-            c.start()
-        lax.fori_loop(32, 40, with_update, 0)
-        late = [out_copy(h * HB + 384, 128, 2 + h) for h in range(2)]
-        for c in late:
-            c.start()
-        for c in early + late:
-            c.wait()
-
+        lax.fori_loop(0, per * (4 + lag), with_update, 0)
         for t in range(4):
             for s in range(2):
                 @pl.when(trees[t].has[s])
                 def _():
-                    ref = big.at[pl.ds(0, 2 * KT * RC)]
+                    ref = big.at[pl.ds(0, HB)]
                     remote(ref, ref, tree_send.at[t, s], lr1.at[0], (row, col)).wait_send()
         for kind in range(3):
             ref = l10.at[pl.ds(0, HB // 2)] if kind == 1 else big.at[pl.ds(0, HB)]
@@ -557,6 +564,15 @@
             @pl.when(jnp.logical_and(zrow, row == other) if kind == 0 else far)
             def _():
                 remote(ref, ref, zsend.at[kind, 1], lr1.at[0], (row, col)).wait_send()
+
+
+    @pl.when(col == 1)
+    def _():
+        trailing(True)
+
+    @pl.when(col > 1)
+    def _():
+        trailing(False)
 
 
 def body(a_window, l_panel, l_inverse):
@@ -565,13 +581,11 @@
     return pl.pallas_call(
         kernel,
         out_shape=jax.ShapeDtypeStruct((W, W), F32),
-        in_specs=[pl.BlockSpec(memory_space=pl.ANY)] * 3,
-        out_specs=pl.BlockSpec(memory_space=pl.ANY),
+        in_specs=[pl.BlockSpec(memory_space=pl.ANY)] * 2 + [pl.BlockSpec(memory_space=pltpu.VMEM)],
+        out_specs=pl.BlockSpec(memory_space=pltpu.VMEM),
         scratch_shapes=[
             vmem((3 * W, W), F32),
             vmem((W, W), F32),
-            vmem((W, W), F32),
-            vmem((2, HB, HB), F32),
             vmem((HB, HB), F32),
             vmem((W, W), F32),
             vmem((W, W), BF16), vmem((W, W), BF16),
@@ -589,10 +603,9 @@
             dma((KZL,)), dma((KZL,)),
             dma((KZ,)), dma((KZ,)),
             dma((3, 4)),
-            dma((4,)),
         ],
         compiler_params=pltpu.CompilerParams(
-            collective_id=0, has_side_effects=True, vmem_limit_bytes=64000000
+            collective_id=0, has_side_effects=True, vmem_limit_bytes=48500000
         ),
         name="block_step",
     )(a_window, l_panel, l_inverse)

time: 115 us -> 95.7 us (0.83)
  Pallas kernels: 110 us -> 92 us
  local copies, waits for them, and re-layouts: 4.79 us -> 3.61 us
    pallas_call x1, Pallas kernels: 110 us -> 92 us  [body(): pl.pallas_call(kernel, out_shape=jax.ShapeDtypeStruct((W, W), F32), in_sp...]
    unnamed x1 -> x3, local copies, waits for them, and re-layouts: 4.79 us -> 3.61 us
where the time goes in v2:
time: 95.7 us; the launch traced here: 95.6 us
  Pallas kernels  92 us (96%)
  local copies, waits for them, and re-layouts  3.61 us (4%)
    pallas_call x1, Pallas kernels, body(): pl.pallas_call(kernel, out_shape=jax.ShapeDtypeStruct((W, W), F32), in_sp...  92 us
    unnamed x3, local copies, waits for them, and re-layouts  3.61 us

profile of v2, /device:TPU:1, one launch (start us, length us, event | category | flops | bytes accessed | tf_op | source)
XLA Modules:
  0.0 95.6 jit_solution(11388197616431474912)
XLA Ops:
  0.0 0.0 copy-start
  0.0 1.6 %copy-done = f32[2,512,512]{2,1,0:T(8,128)S(1)} copy-done((f32[2,512,512]{2,1,0:T(8,128)S(1)}, f32[2,512,512]{2,1,0:T(8,128)}, u32[]{:S(2)}) %copy-start) | copy-done | bytes 2097176
  1.6 92.0 %block_step.1 = f32[1024,1024]{1,0:T(8,128)S(1)} custom-call(f32[1024,1024]{1,0:T(8,128)} %a_hbm.1, f32[1024,1024]{1,0:T(8,128)} %l_hbm.1, f32[2,512,512]{2,1,0:T(8,128)S(1)} %copy-done), custom_call_target="tpu_custom_call" | custom-call | tf_op jit(solution)/shard_map/block_step/pallas_call | solution.py:581
  93.6 2.0 %copy.5 = f32[1024,1024]{1,0:T(8,128)} copy(f32[1024,1024]{1,0:T(8,128)S(1)} %block_step.1) | data formatting | bytes 8388608
Async XLA Ops:
  0.0 1.6 %copy-start = (f32[2,512,512]{2,1,0:T(8,128)S(1)}, f32[2,512,512]{2,1,0:T(8,128)}, u32[]{:S(2)}) copy-start(f32[2,512,512]{2,1,0:T(8,128)} %inv.1) | copy-start | bytes 6291460

commit v3 on v2

--- a/solution.py
+++ b/solution.py
@@ -28,7 +28,7 @@
 ZL0 = 36
 ZG0 = 62
 DEEP = 6
-HOLD = 56
+HOLD = 48
 
 
 def split(v):
@@ -387,10 +387,9 @@
         kt = W // (4 * rc)
         zl0, zg0 = (4, 30) if one else (ZL0, ZG0)
         have_l = zl0 + KZL + (SD if one else 3 * SZ + SD)
-        begin = kt + kt // 4 + sig * DEEP
-        lag = 0 if one else 1
         per = kt // 4
-        a_at, g_at = ((0, 1), (2, 3)) if one else ((1, 3), (5, 7))
+        begin = (per if one else kt + per) + sig * DEEP
+        a_at, g_at = (1, 2) if one else (1, 3), (5, 7)
 
         @pl.when(mine)
         def _():
@@ -476,7 +475,7 @@
                 @pl.when(jnp.logical_and(k >= 0, k < 2 * kt))
                 def _():
                     m, i = lax.div(k, kt), lax.rem(k, kt)
-                    at = m * W + (t // 2) * HB + i * 2 * rc + (t % 2) * rc
+                    at = (1 - m if one else m) * W + (t // 2) * HB + i * 2 * rc + (t % 2) * rc
                     tree_step(t, k, at, big, rc, tree_send)
 
         def comm_only(s, _):
@@ -497,8 +496,8 @@
             return 0
 
         lax.fori_loop(0, 4, with_p, 0)
-        assert have_l + 12 <= begin
-        lax.fori_loop(have_l + 8, begin - 4, comm_only, 0)
+        assert have_l + (8 if one else 12) <= begin
+        lax.fori_loop(have_l + 8, begin - (0 if one else 4), comm_only, 0)
         load_u.wait()
 
         def split_l(i, _):
@@ -511,7 +510,15 @@
                 ll[:, cols] = l
             return 0
 
-        lax.fori_loop(0, 4, split_l, 0)
+        if not one:
+            lax.fori_loop(0, 4, split_l, 0)
+
+        def split_g(g):
+            for j in range(2):
+                rows = pl.ds(pl.multiple_of(j * HB + g * 128, 128), 128)
+                h, l = split(gbuf[rows])
+                ph[rows] = h
+                plo[rows] = l
 
         def with_update(v, _):
             slot(begin + v)
@@ -534,20 +541,50 @@
                     part = jnp.where(top, 0.0, upd[:, j * 128:j * 128 + 128])
                     u[rows, cols] = u[rows, cols] - part
 
-            gb = b - lag
-
-            @pl.when(jnp.logical_and(jnp.logical_or(w == g_at[0], w == g_at[1]), gb >= 0))
-            def _():
-                at = jnp.where(w == g_at[1], HB, 0) + gb * 128
-                rows = pl.ds(pl.multiple_of(at, 128), 128)
-                g = split(gbuf[rows])
+            if one:
+                @pl.when(jnp.logical_and(w == 0, b >= 4))
+                def _():
+                    for j in range(2):
+                        at = j * HB + (b - 4) * 128
+                        cols = pl.ds(pl.multiple_of((b - 4) * 256 + j * 128, 128), 128)
+                        h, l = split(big[pl.ds(pl.multiple_of(at, 128), 128)].T)
+                        lh[:, cols] = h
+                        ll[:, cols] = l
+
+                @pl.when(jnp.logical_and(w == 1, jnp.logical_and(b >= 4, b < 7)))
+                def _():
+                    split_g(b - 4)
+            else:
+                gb = b - 1
+
+                @pl.when(jnp.logical_and(jnp.logical_or(w == g_at[0], w == g_at[1]), gb >= 0))
+                def _():
+                    at = jnp.where(w == g_at[1], HB, 0) + gb * 128
+                    rows = pl.ds(pl.multiple_of(at, 128), 128)
+                    g = split(gbuf[rows])
+                    for j in range(2):
+                        cols = slice(j * HB, j * HB + HB)
+                        upd = mul3(g, (lh[:, cols], ll[:, cols]))
+                        u[rows, cols] = u[rows, cols] - jnp.where(top, 0.0, upd)
+            return 0
+
+        lax.fori_loop(0, per * (8 if one else 5), with_update, 0)
+
+        if one:
+            split_g(3)
+
+            def g_update(i, _):
+                n, h = lax.div(i, 2), lax.rem(i, 2)
+                rows = pl.ds(pl.multiple_of(h * HB, HB), HB)
+                cols = pl.ds(pl.multiple_of(n * 256, 256), 256)
+                upd = mul3((ph[rows], plo[rows]), (lh[:, cols], ll[:, cols]))
                 for j in range(2):
-                    cols = slice(j * HB, j * HB + HB)
-                    upd = mul3(g, (lh[:, cols], ll[:, cols]))
-                    u[rows, cols] = u[rows, cols] - jnp.where(top, 0.0, upd)
-            return 0
-
-        lax.fori_loop(0, per * (4 + lag), with_update, 0)
+                    at = pl.ds(pl.multiple_of(j * HB + n * 128, 128), 128)
+                    part = jnp.where(top, 0.0, upd[:, j * 128:j * 128 + 128])
+                    u[rows, at] = u[rows, at] - part
+                return 0
+
+            lax.fori_loop(0, 8, g_update, 0)
         for t in range(4):
             for s in range(2):
                 @pl.when(trees[t].has[s])

time: 95.7 us -> 92.5 us (0.967)
  the two profiles are of different devices: /device:TPU:1 before, /device:TPU:32 now
where the time goes in v3:
time: 92.5 us; the launch traced here: 92.3 us
  Pallas kernels  88.7 us (96%)
  local copies, waits for them, and re-layouts  3.61 us (4%)
    pallas_call x1, Pallas kernels, body(): pl.pallas_call(kernel, out_shape=jax.ShapeDtypeStruct((W, W), F32), in_sp...  88.7 us
    unnamed x3, local copies, waits for them, and re-layouts  3.61 us

profile of v3, /device:TPU:32, one launch (start us, length us, event | category | flops | bytes accessed | tf_op | source)
XLA Modules:
  0.0 92.3 jit_solution(46000828814868657)
XLA Ops:
  0.0 0.0 copy-start
  0.0 1.6 %copy-done = f32[2,512,512]{2,1,0:T(8,128)S(1)} copy-done((f32[2,512,512]{2,1,0:T(8,128)S(1)}, f32[2,512,512]{2,1,0:T(8,128)}, u32[]{:S(2)}) %copy-start) | copy-done | bytes 2097176
  1.6 88.7 %block_step.1 = f32[1024,1024]{1,0:T(8,128)S(1)} custom-call(f32[1024,1024]{1,0:T(8,128)} %a_hbm.1, f32[1024,1024]{1,0:T(8,128)} %l_hbm.1, f32[2,512,512]{2,1,0:T(8,128)S(1)} %copy-done), custom_call_target="tpu_custom_call" | custom-call | tf_op jit(solution)/shard_map/block_step/pallas_call | solution.py:618
  90.3 2.0 %copy.5 = f32[1024,1024]{1,0:T(8,128)} copy(f32[1024,1024]{1,0:T(8,128)S(1)} %block_step.1) | data formatting | bytes 8388608
Async XLA Ops:
  0.0 1.6 %copy-start = (f32[2,512,512]{2,1,0:T(8,128)S(1)}, f32[2,512,512]{2,1,0:T(8,128)}, u32[]{:S(2)}) copy-start(f32[2,512,512]{2,1,0:T(8,128)} %inv.1) | copy-start | bytes 6291460

commit v4 on v3

--- a/solution.py
+++ b/solution.py
@@ -532,9 +532,9 @@
                     ah[:, j * 128:j * 128 + 128] = h
                     al[:, j * 128:j * 128 + 128] = l
 
-            @pl.when(jnp.logical_and(jnp.logical_or(w == a_at[0], w == a_at[1]), b < 4))
-            def _():
-                rows = pl.ds(pl.multiple_of(jnp.where(w == a_at[1], HB, 0), HB), HB)
+            @pl.when(jnp.logical_and(w == a_at[0], b < 4))
+            def _():
+                rows = pl.ds(0, W)
                 upd = mul3((ph[rows], plo[rows]), (ah[:, 0:256], al[:, 0:256]))
                 for j in range(2):
                     cols = pl.ds(pl.multiple_of(j * HB + b * 128, 128), 128)

time: 92.5 us -> 94.6 us (1.023)
  the two profiles are of different devices: /device:TPU:32 before, /device:TPU:97 now
where the time goes in v4:
time: 94.6 us; the launch traced here: 94.5 us
  Pallas kernels  90.9 us (96%)
  local copies, waits for them, and re-layouts  3.61 us (4%)
    pallas_call x1, Pallas kernels, body(): pl.pallas_call(kernel, out_shape=jax.ShapeDtypeStruct((W, W), F32), in_sp...  90.9 us
    unnamed x3, local copies, waits for them, and re-layouts  3.61 us

profile of v4, /device:TPU:97, one launch (start us, length us, event | category | flops | bytes accessed | tf_op | source)
XLA Modules:
  0.0 94.5 jit_solution(17525689449214511264)
XLA Ops:
  0.0 0.0 copy-start
  0.0 1.6 %copy-done = f32[2,512,512]{2,1,0:T(8,128)S(1)} copy-done((f32[2,512,512]{2,1,0:T(8,128)S(1)}, f32[2,512,512]{2,1,0:T(8,128)}, u32[]{:S(2)}) %copy-start) | copy-done | bytes 2097176
  1.6 90.9 %block_step.1 = f32[1024,1024]{1,0:T(8,128)S(1)} custom-call(f32[1024,1024]{1,0:T(8,128)} %a_hbm.1, f32[1024,1024]{1,0:T(8,128)} %l_hbm.1, f32[2,512,512]{2,1,0:T(8,128)S(1)} %copy-done), custom_call_target="tpu_custom_call" | custom-call | tf_op jit(solution)/shard_map/block_step/pallas_call | solution.py:618
  92.5 2.0 %copy.5 = f32[1024,1024]{1,0:T(8,128)} copy(f32[1024,1024]{1,0:T(8,128)S(1)} %block_step.1) | data formatting | bytes 8388608
Async XLA Ops:
  0.0 1.6 %copy-start = (f32[2,512,512]{2,1,0:T(8,128)S(1)}, f32[2,512,512]{2,1,0:T(8,128)}, u32[]{:S(2)}) copy-start(f32[2,512,512]{2,1,0:T(8,128)} %inv.1) | copy-start | bytes 6291460
